TPU v7x, 32 devices: a whole 2x2x4 slice. The times are simulated.
32 devices in a mesh: band: 8 (over z, y), field: 4 (over x, core).
Axes of the slice: x: 2, y: 2, z: 4, core: 2. Of those that a mesh axis runs over, the one named last changes fastest.
Arguments:
- right_side: float32 [640, 2, 4, 12, 640], P('band', None, 'field'), may hold values from -40 to 40
- legendre: bfloat16 [640, 640, 640], P('band'), may hold values from -0.25 to 0.25
- wave_map: int32 [640], replicated, may hold values from 0 to 639, as said below
- obs_weight: float32 [640, 1280], P('band'), may hold values from 0.2 to 5
Outputs:
- solution: float32 [640, 2, 4, 12, 640], P('band', None, 'field')
- residual: float32 [640, 2, 4, 12, 640], P('band', None, 'field')
Inputs may be any that keep to these rules, and one draw needn't show every extreme that they name: A permutation of 0 to 639; wave_map[s] lies in the same aligned block of 20 values as 639-s.
All inputs are finite; a program needn't handle non-finite values.
Results may differ from a plain program's by a relative error of at most 0.03.
Values may be sent and summed in bfloat16 or wider, within the bound.
A program may use at most 192 MiB of HBM per device.

v0:
```python
import math

import jax
import jax.numpy as jnp
from jax import lax
from jax.sharding import PartitionSpec as P

ITERS = 3


def triangle_of(own_waves, degrees):
    return (jnp.arange(degrees, dtype=jnp.int32)[None, :] >= own_waves[:, None]).astype(jnp.float32)


def fourier_of(wave_map, lon_count):
    longitude = jnp.arange(lon_count, dtype=jnp.int32)
    phase_int = wave_map[:, None] * longitude[None, :] % lon_count
    angles = phase_int.astype(jnp.float32) * (2.0 * math.pi / lon_count)
    norm_factor = 1.0 / math.sqrt(wave_map.shape[0])
    return (jnp.stack([jnp.cos(angles), -jnp.sin(angles)], axis=1) * norm_factor).astype(
        jnp.bfloat16
    )


def grid_round(spread, fourier_flat, obs_weight):
    slots, parts, items, single, lat_rows = spread.shape
    flat = spread.reshape(slots * parts, items * single * lat_rows)
    grid_vals = lax.dot_general(
        flat, fourier_flat, (((0,), (0,)), ((), ())), preferred_element_type=jnp.float32
    )
    grid_vals = (
        grid_vals.reshape(items * single, lat_rows, fourier_flat.shape[1]) * obs_weight[None, :, :]
    )
    weighted = grid_vals.astype(jnp.bfloat16).reshape(
        items * single * lat_rows, fourier_flat.shape[1]
    )
    returned = lax.dot_general(
        fourier_flat, weighted, (((1,), (1,)), ((), ())), preferred_element_type=jnp.float32
    ).astype(jnp.bfloat16)
    return returned.reshape(slots, parts, items, single, lat_rows)


def legendre_back(returned, legendre):
    return lax.dot_general(
        returned, legendre, (((4,), (2,)), ((0,), (0,))), preferred_element_type=jnp.float32
    )


def paired_sums(residual, image_vec):
    return lax.psum(
        (jnp.sum(residual * residual), jnp.sum(residual * image_vec)), ("band", "field")
    )


def on_device(right_side, legendre, wave_map, obs_weight):
    slot_count = legendre.shape[0]
    band_count = lax.axis_size("band")
    lat_rows = obs_weight.shape[0]
    first_slot = lax.axis_index("band") * slot_count
    own_waves = lax.dynamic_slice_in_dim(wave_map, first_slot, slot_count)
    triangle = triangle_of(own_waves, right_side.shape[4])
    fourier_table = fourier_of(wave_map, obs_weight.shape[1])
    fourier_flat = fourier_table.reshape(2 * fourier_table.shape[0], fourier_table.shape[2])
    triangle_five = triangle[:, None, None, None, :]
    field_count = right_side.shape[2]
    level_count = right_side.shape[3]
    merged = field_count * level_count

    def operate(vector):
        masked_bf = (vector * triangle_five).astype(jnp.bfloat16)
        coeffs = lax.dot_general(
            masked_bf, legendre, (((4,), (1,)), ((0,), (0,))), preferred_element_type=jnp.float32
        ).astype(jnp.bfloat16)
        outgoing = coeffs.reshape(slot_count, 2, merged, band_count, lat_rows)
        spread = lax.all_to_all(outgoing, "band", split_axis=3, concat_axis=0, tiled=True)
        returned = grid_round(spread, fourier_flat, obs_weight)
        returned_home = lax.all_to_all(returned, "band", split_axis=0, concat_axis=3, tiled=True)
        home = returned_home.reshape(slot_count, 2, field_count, level_count, band_count * lat_rows)
        adjoint = legendre_back(home, legendre)
        return vector + triangle_five * adjoint

    residual = right_side * triangle_five
    solution = jnp.zeros_like(residual)
    image_vec = operate(residual)
    norm_now, product = paired_sums(residual, image_vec)
    step_length = norm_now / product
    direction = residual
    along = image_vec
    for iteration in range(ITERS):
        solution = solution + step_length * direction
        residual = residual - step_length * along
        if iteration + 1 < ITERS:
            image_vec = operate(residual)
            norm_next, product = paired_sums(residual, image_vec)
            beta_ratio = norm_next / norm_now
            step_length = norm_next / (product - beta_ratio * norm_next / step_length)
            direction = residual + beta_ratio * direction
            along = image_vec + beta_ratio * along
            norm_now = norm_next
    return (solution, residual)


def solution(mesh):
    in_specs = (P("band", None, "field", None, None), P("band", None, None), P(), P("band", None))
    out_specs = (P("band", None, "field", None, None), P("band", None, "field", None, None))
    return jax.shard_map(
        on_device, mesh=mesh, in_specs=in_specs, out_specs=out_specs, check_vma=False
    )
```

profile of v0, /device:TPU:8, one launch (start us, length us, event | category | flops | bytes accessed | tf_op | source)
XLA Modules:
  0.0 1089.4 jit_solution(2775460393067917803)
XLA Ops:
  1.5 24.8 %fusion.43 = bf16[80,2,12,640]{3,2,1,0:T(8,128)(2,1)S(1)} fusion(bf16[80,640,640]{2,1,0:T(8,128)(2,1)} %param.5, f32[80,2,1,12,640]{4,2,3,1,0:T(1,128)} %param.4, f32[80,640]{1,0:T(8,128)S(1)} %fusion.58), kind=kOutput, calls=%fused_computation.66 | convolution fusion | flops 1577779200 | bytes 73113600 | tf_op jit(solution)/shard_map/dot_general | solution.py:71
  26.3 5.2 reshape.240
  31.5 6.6 copy.90
  38.0 6.9 all-to-all-start
  44.9 13.6 %fusion.38 = (f32[640,1,1280]{2,0,1:T(8,128)S(1)}, f32[640,1,1280]{2,0,1:T(8,128)S(1)}) fusion(s32[640]{0:T(1024)S(1)} %copy-done.3), kind=kLoop, calls=%fused_computation.61 | loop fusion | flops 8192000 | bytes 6556160 | tf_op jit(solution)/shard_map/cos | solution.py:20
  69.1 60.4 %all-to-all-done = bf16[80,2,12,8,80]{4,0,2,1,3:T(8,128)(2,1)} async-done(((bf16[80,2,12,8,80]{4,0,2,1,3:T(8,128)(2,1)}), bf16[80,2,12,8,80]{4,0,2,1,3:T(8,128)(2,1)}, u32[]{:S(2)}, u32[]{:S(2)}) %all-to-all-start) | async-done | bytes 2457632 | tf_op jit(solution)/shard_map/all_to_all | solution.py:75
  129.6 5.7 copy.91
  135.2 7.3 reshape.222
  145.2 6.2 multiply_convert_fusion.4
  151.3 4.9 convolution_convert_fusion.2
  159.2 7.2 reshape.224
  166.4 8.4 copy.94
  174.8 93.2 %all_to_all.90 = bf16[640,2,12,1,80]{4,1,3,2,0:T(2,128)(2,1)S(1)} all-to-all(bf16[640,2,12,1,80]{4,1,3,2,0:T(2,128)(2,1)} %copy.94), channel_id=1, replica_groups=mesh['band'=8,'field'=4] {'band'}, dimensions={0} | all-to-all | bytes 4915200 | tf_op jit(solution)/shard_map/all_to_all | solution.py:77
  268.1 4.5 copy.196
  272.5 5.5 reshape.225
  278.0 30.5 %fusion.21 = (f32[]{:T(128)}, f32[]{:T(128)}, f32[80,2,12,640]{3,2,1,0:T(8,128)}) fusion(f32[80,2,1,12,640]{4,2,3,1,0:T(1,128)} %param.4, f32[80,640]{1,0:T(8,128)S(1)} %fusion.58, bf16[80,640,640]{2,1,0:T(8,128)(2,1)} %param.5, bf16[80,2,12,640]{3,0,2,1:T(8,128)(2,1)S(1)} %reshape.225), kind=kOutput, calls=%fused_computation.26 | convolution fusion | flops 1581465600 | bytes 78028808 | tf_op jit(solution)/shard_map/dot_general | solution.py:44
  308.5 40.2 %all-reduce.2 = (f32[]{:T(128)}, f32[]{:T(128)}) all-reduce(f32[]{:T(128)} %get-tuple-element.17, f32[]{:T(128)} %get-tuple-element.16), channel_id=1, replica_groups=mesh['band'=8,'field'=4] {'band','field'}, use_global_device_ids=true, to_apply=%region_1.2 | all-reduce | flops 2 | bytes 16 | tf_op jit(solution)/shard_map/psum | solution.py:50
  350.1 26.1 %fusion.48 = bf16[80,2,12,640]{3,2,1,0:T(8,128)(2,1)S(1)} fusion(bf16[80,640,640]{2,1,0:T(8,128)(2,1)} %param.5, f32[80,640]{1,0:T(8,128)S(1)} %fusion.58, f32[80,2,1,12,640]{4,2,3,1,0:T(1,128)} %param.4, f32[80,2,12,640]{3,2,1,0:T(8,128)} %get-tuple-element.28, f32[]{:T(128)S(6)} %div.21), kind=kOutput, calls=%fused_computation.67 | convolution fusion | flops 1582694400 | bytes 78028800 | tf_op jit(solution)/shard_map/dot_general | solution.py:71
  376.1 5.2 reshape.242
  381.3 4.6 copy.98
  386.0 90.8 %all_to_all.91 = bf16[80,2,12,8,80]{4,0,2,1,3:T(8,128)(2,1)S(1)} all-to-all(bf16[80,2,12,8,80]{4,0,2,1,3:T(8,128)(2,1)S(1)} %copy.98), channel_id=1, replica_groups=mesh['band'=8,'field'=4] {'band'}, dimensions={3} | all-to-all | bytes 4915200 | tf_op jit(solution)/shard_map/all_to_all | solution.py:75
  480.4 7.3 reshape.228
  490.3 6.2 multiply_convert_fusion.3
  496.5 4.7 convolution_convert_fusion.1
  504.1 7.2 reshape.230
  511.3 8.4 copy.102
  519.8 91.3 %all_to_all.92 = bf16[640,2,12,1,80]{4,1,3,2,0:T(2,128)(2,1)S(1)} all-to-all(bf16[640,2,12,1,80]{4,1,3,2,0:T(2,128)(2,1)} %copy.102), channel_id=1, replica_groups=mesh['band'=8,'field'=4] {'band'}, dimensions={0} | all-to-all | bytes 4915200 | tf_op jit(solution)/shard_map/all_to_all | solution.py:77
  611.0 4.5 copy.195
  615.5 5.5 reshape.231
  621.0 31.8 %multiply_reduce_fusion.2 = (f32[]{:T(128)}, f32[]{:T(128)}, f32[80,2,12,640]{3,2,1,0:T(8,128)}) fusion(f32[80,640]{1,0:T(8,128)S(1)} %fusion.58, f32[80,2,12,640]{3,2,1,0:T(8,128)} %get-tuple-element.28, f32[]{:T(128)S(6)} %div.21, f32[80,2,1,12,640]{4,2,3,1,0:T(1,128)} %param.4, bf16[80,640,640]{2,1,0:T(8,128)(2,1)} %param.5, ...), kind=kOutput, calls=%fused_computation.36 | convolution fusion | flops 1586380800 | bytes 82944016 | tf_op jit(solution)/shard_map/dot_general | solution.py:44
  652.8 39.0 %all-reduce.1 = (f32[]{:T(128)}, f32[]{:T(128)}) all-reduce(f32[]{:T(128)} %get-tuple-element.13, f32[]{:T(128)} %get-tuple-element.12), channel_id=1, replica_groups=mesh['band'=8,'field'=4] {'band','field'}, use_global_device_ids=true, to_apply=%region_5.6 | all-reduce | flops 2 | bytes 16 | tf_op jit(solution)/shard_map/psum | solution.py:50
  696.5 10.1 multiply_subtract_fusion.1
  706.7 25.3 %fusion.53 = bf16[80,2,12,640]{3,2,1,0:T(8,128)(2,1)S(1)} fusion(bf16[80,640,640]{2,1,0:T(8,128)(2,1)} %param.5, f32[80,2,1,12,640]{4,3,1,0,2:T(8,128)} %multiply_subtract_fusion.1, f32[80,640]{1,0:T(8,128)S(1)} %fusion.58), kind=kOutput, calls=%fused_computation.68 | convolution fusion | flops 1576550400 | bytes 73113600 | tf_op jit(solution)/shard_map/dot_general | solution.py:71
  732.0 5.2 reshape.243
  737.2 4.6 copy.106
  741.8 91.0 %all_to_all.93 = bf16[80,2,12,8,80]{4,0,2,1,3:T(8,128)(2,1)S(1)} all-to-all(bf16[80,2,12,8,80]{4,0,2,1,3:T(8,128)(2,1)S(1)} %copy.106), channel_id=1, replica_groups=mesh['band'=8,'field'=4] {'band'}, dimensions={3} | all-to-all | bytes 4915200 | tf_op jit(solution)/shard_map/all_to_all | solution.py:75
  836.3 7.3 reshape.234
  846.2 6.2 multiply_convert_fusion.2
  852.4 4.7 convolution_convert_fusion
  860.1 7.2 reshape.236
  867.2 8.4 copy.110
  875.7 90.9 %all_to_all.94 = bf16[640,2,12,1,80]{4,1,3,2,0:T(2,128)(2,1)S(1)} all-to-all(bf16[640,2,12,1,80]{4,1,3,2,0:T(2,128)(2,1)} %copy.110), channel_id=1, replica_groups=mesh['band'=8,'field'=4] {'band'}, dimensions={0} | all-to-all | bytes 4915200 | tf_op jit(solution)/shard_map/all_to_all | solution.py:77
  971.1 5.5 reshape.237
  976.6 31.0 %multiply_reduce_fusion = (f32[]{:T(128)}, f32[]{:T(128)}, f32[80,2,12,640]{3,2,1,0:T(8,128)}) fusion(f32[80,2,1,12,640]{4,3,1,0,2:T(8,128)} %multiply_subtract_fusion.1, f32[80,640]{1,0:T(8,128)S(1)} %fusion.58, bf16[80,640,640]{2,1,0:T(8,128)(2,1)} %param.5, bf16[80,2,12,640]{3,0,2,1:T(8,128)(2,1)S(1)} %reshape.237), kind=kOutput, calls=%fused_computation.31 | convolution fusion | flops 1580236800 | bytes 78028808 | tf_op jit(solution)/shard_map/dot_general | solution.py:44
  1007.5 39.4 %all-reduce = (f32[]{:T(128)}, f32[]{:T(128)}) all-reduce(f32[]{:T(128)} %get-tuple-element.15, f32[]{:T(128)} %get-tuple-element.14), channel_id=1, replica_groups=mesh['band'=8,'field'=4] {'band','field'}, use_global_device_ids=true, to_apply=%region_9.10 | all-reduce | flops 2 | bytes 16 | tf_op jit(solution)/shard_map/psum | solution.py:50
  1051.0 17.7 %multiply_subtract_fusion = (f32[80,2,1,12,640]{4,3,1,0,2:T(8,128)}, f32[80,2,1,12,640]{4,3,1,0,2:T(8,128)}) fusion(f32[80,2,1,12,640]{4,3,1,0,2:T(8,128)} %multiply_subtract_fusion.1, f32[80,2,12,640]{3,2,1,0:T(8,128)} %get-tuple-element.30, f32[]{:T(128)S(6)} %div.25, f32[]{:T(128)S(6)} %div.27, f32[80,640]{1,0:T(8,128)S(1)} %fusion.58, ...), kind=kLoop, calls=%fused_computation.30 | loop fusion | flops 29491200 | bytes 34611220 | tf_op jit(solution)/shard_map/sub | solution.py:91
  1068.6 10.2 copy.114
  1078.8 10.2 copy.113
  (29 shorter events, 39.9 us)
Async XLA Ops:
  38.0 6.9 copy-start.3
  38.0 91.5 %all-to-all-start = ((bf16[80,2,12,8,80]{4,0,2,1,3:T(8,128)(2,1)}), bf16[80,2,12,8,80]{4,0,2,1,3:T(8,128)(2,1)}, u32[]{:S(2)}, u32[]{:S(2)}) async-start(bf16[80,2,12,8,80]{4,0,2,1,3:T(8,128)(2,1)} %copy.90), calls=%async_computation | async-start | bytes 7864320 | tf_op jit(solution)/shard_map/all_to_all | solution.py:75
  135.2 9.9 copy-start.4
  145.2 6.2 copy-start
  480.4 9.9 copy-start.5
  490.3 6.2 copy-start.1
  836.3 9.9 copy-start.6
  846.2 6.2 copy-start.2
where the time goes:
time: 1100 us; the launch traced here: 1090 us
  blocking collectives  576 us (52%)
  matrix products  202 us (18%)
  local copies, waits for them, and re-layouts  191 us (17%)
  waiting for transfers between devices  60.4 us (5%)
  other arithmetic  42.1 us (4%)
  between operations  11.4 us (1%)
    all_to_all x3, blocking collectives, operate(): lax.all_to_all(returned, 'band', split_axis=0, concat_axis=3, tiled=True)  275 us
    all_to_all x2, blocking collectives, operate(): lax.all_to_all(outgoing, 'band', split_axis=3, concat_axis=0, tiled=True)  182 us
    psum x3, blocking collectives, paired_sums(): lax.psum((jnp.sum(residual * residual), jnp.sum(residual * image_vec)), (...  119 us
    dot_general x3, matrix products, legendre_back(): lax.dot_general(returned, legendre, (((4,), (2,)), ((0,), (0,))), preferr...  93.3 us
    dot_general x3, matrix products, operate(): lax.dot_general(masked_bf, legendre, (((4,), (1,)), ((0,), (0,))), prefer...  76.1 us
    all_to_all x1, waiting for transfers between devices, operate(): lax.all_to_all(outgoing, 'band', split_axis=3, concat_axis=0, tiled=True)  60.4 us
    reshape x6, local copies, waits for them, and re-layouts, grid_round(): return returned.reshape(slots, parts, items, single, lat_rows)  46.9 us
    reshape x6, local copies, waits for them, and re-layouts, operate(): outgoing = coeffs.reshape(slot_count, 2, merged, band_count, lat_rows)  31.5 us
  transfers between devices with their start and end apart: 1, of which 1 were waited for; matrix products, arithmetic and copies ran while one was open for 2% of the time, Pallas kernels for 0%

commit v1 on v0

--- a/solution.py
+++ b/solution.py
@@ -100,9 +100,123 @@
     return (solution, residual)
 
 
+LANES = 128
+
+
+def tiled_split(levels, lat_count, band_count):
+    tiles = lat_count // LANES
+    return lat_count % LANES == 0 and tiles % 2 == 1 and 2 * levels == 3 * band_count
+
+
+def fourier_phase(phase_int, lon_count, slot_total, part_axis):
+    angles = phase_int.astype(jnp.float32) * (2.0 * math.pi / lon_count)
+    norm_factor = 1.0 / math.sqrt(slot_total)
+    return (jnp.stack([jnp.cos(angles), -jnp.sin(angles)], axis=part_axis) * norm_factor).astype(
+        jnp.bfloat16
+    )
+
+
+def on_device_tiled(right_side, legendre, wave_map, obs_weight):
+    slot_count, parts, field_count, level_count, degrees = right_side.shape
+    band_count = lax.axis_size("band")
+    levels = field_count * level_count
+    lat_count = legendre.shape[2]
+    lon_count = obs_weight.shape[1]
+    slot_total = wave_map.shape[0]
+    groups = band_count // 2
+    shared = (lat_count // LANES + 1) // 2 * LANES
+    width = lat_count + shared
+    tail_from = lat_count - shared
+    band_at = lax.axis_index("band")
+    odd = band_at % 2
+    own_waves = lax.dynamic_slice_in_dim(wave_map, band_at * slot_count, slot_count)
+    triangle = triangle_of(own_waves, degrees)[:, None, :]
+
+    longitude = jnp.arange(lon_count, dtype=jnp.int32)
+    waves = wave_map.reshape(band_count, slot_count)
+    rows_phase = waves[:, :, None] * longitude[None, None, :] % lon_count
+    table = fourier_phase(rows_phase, lon_count, slot_total, 1)
+    table = table.reshape(parts * slot_total, lon_count)
+    cols_phase = longitude[:, None, None] * waves[None, :, :] % lon_count
+    table_t = fourier_phase(cols_phase, lon_count, slot_total, 2)
+    table_t = table_t.reshape(lon_count, parts * slot_total)
+    table, table_t = lax.optimization_barrier((table, table_t))
+
+    weight_all = lax.all_gather(obs_weight, "band", axis=0, tiled=True)
+    weight_tail = lax.dynamic_slice_in_dim(weight_all, odd * tail_from, shared)
+    weight_t = jnp.concatenate([weight_all, weight_tail], axis=0).T
+    weight_t = lax.optimization_barrier(weight_t)
+    column = jnp.arange(width, dtype=jnp.int32)
+    twice = (column >= lat_count) & (column < lat_count + LANES) & (odd == 1)
+    counted = jnp.where(twice, 0.0, 1.0).astype(jnp.float32)
+
+    def operate(vector):
+        masked_bf = (vector * triangle).astype(jnp.bfloat16)
+        coeffs = lax.dot_general(
+            masked_bf, legendre, (((2,), (1,)), ((0,), (0,))), preferred_element_type=jnp.float32
+        ).astype(jnp.bfloat16)
+        planes = coeffs.reshape(slot_count, parts, levels, lat_count).transpose(2, 1, 0, 3)
+        planes = planes.reshape(groups, 3, parts * slot_count, lat_count)
+        first = jnp.concatenate([planes[:, 0], planes[:, 1, :, :shared]], axis=2)
+        second = jnp.concatenate([planes[:, 2], planes[:, 1, :, tail_from:]], axis=2)
+        outgoing = jnp.stack([first, second], axis=1)
+        outgoing = outgoing.reshape(band_count, parts * slot_count, width)
+        spread = lax.all_to_all(outgoing, "band", split_axis=0, concat_axis=0, tiled=True)
+        spread = spread.reshape(parts * slot_total, width)
+        grid_t = lax.dot_general(
+            table_t, spread, (((1,), (0,)), ((), ())), preferred_element_type=jnp.float32
+        )
+        weighted = grid_t * weight_t
+        energy = jnp.sum(weighted * grid_t * counted[None, :])
+        weighted_bf = weighted.astype(jnp.bfloat16)
+        returned = lax.dot_general(
+            table, weighted_bf, (((1,), (0,)), ((), ())), preferred_element_type=jnp.float32
+        ).astype(jnp.bfloat16)
+        returned = returned.reshape(band_count, parts * slot_count, width)
+        sums = lax.psum((jnp.sum(vector * vector), energy), "field")
+        norm, product = lax.psum(sums, "band")
+        back = lax.all_to_all(returned, "band", split_axis=0, concat_axis=0, tiled=True)
+        back = back.reshape(groups, 2, parts * slot_count, width)
+        middle = jnp.concatenate(
+            [back[:, 0, :, lat_count:], back[:, 1, :, lat_count + LANES :]], axis=2
+        )
+        home = jnp.stack([back[:, 0, :, :lat_count], middle, back[:, 1, :, :lat_count]], axis=1)
+        home = home.reshape(levels, parts, slot_count, lat_count).transpose(2, 1, 0, 3)
+        home = home.reshape(slot_count, parts * levels, lat_count)
+        adjoint = lax.dot_general(
+            home, legendre, (((2,), (2,)), ((0,), (0,))), preferred_element_type=jnp.float32
+        )
+        return vector + triangle * adjoint, norm, norm + product
+
+    residual = right_side.reshape(slot_count, parts * levels, degrees) * triangle
+    image_vec, norm_now, product = operate(residual)
+    step_length = norm_now / product
+    direction = residual
+    along = image_vec
+    solution = step_length * direction
+    residual = residual - step_length * along
+    for iteration in range(1, ITERS):
+        image_vec, norm_next, product = operate(residual)
+        beta_ratio = norm_next / norm_now
+        step_length = norm_next / (product - beta_ratio * norm_next / step_length)
+        direction = residual + beta_ratio * direction
+        along = image_vec + beta_ratio * along
+        norm_now = norm_next
+        solution = solution + step_length * direction
+        residual = residual - step_length * along
+    return solution.reshape(right_side.shape), residual.reshape(right_side.shape)
+
+
+def on_device_any(right_side, legendre, wave_map, obs_weight):
+    levels = right_side.shape[2] * right_side.shape[3]
+    if tiled_split(levels, legendre.shape[2], lax.axis_size("band")):
+        return on_device_tiled(right_side, legendre, wave_map, obs_weight)
+    return on_device(right_side, legendre, wave_map, obs_weight)
+
+
 def solution(mesh):
     in_specs = (P("band", None, "field", None, None), P("band", None, None), P(), P("band", None))
     out_specs = (P("band", None, "field", None, None), P("band", None, "field", None, None))
     return jax.shard_map(
-        on_device, mesh=mesh, in_specs=in_specs, out_specs=out_specs, check_vma=False
-    )
+        on_device_any, mesh=mesh, in_specs=in_specs, out_specs=out_specs, check_vma=False
+    )

time: 1100 us -> 716 us (0.65)
  blocking collectives: 576 us -> 322 us
  local copies, waits for them, and re-layouts: 191 us -> 45.3 us
  waiting for transfers between devices: 60.4 us -> 18.6 us
  other arithmetic: 42.1 us -> 69.3 us
  starting transfers between devices: 6.85 us -> 22.4 us
  between operations: 11.4 us -> 25.2 us
    all_to_all x5 -> x2, blocking collectives: 457 us -> 121 us  [operate(): lax.all_to_all(outgoing, 'band', split_axis=0, concat_axis=0, tiled=True)]
    reshape x15 -> x1, local copies, waits for them, and re-layouts: 100 us -> 6.68 us  [on_device_tiled(): right_side.reshape(slot_count, parts * levels, degrees) * triangle]
    psum x3 -> x6, blocking collectives: 119 us -> 201 us  [the longest x3 182 us: operate(): norm, product = lax.psum(sums, 'band')]
    all_to_all x1 -> x4, waiting for transfers between devices: 60.4 us -> 17.9 us  [the longest x1 17.9 us: operate(): lax.all_to_all(outgoing, 'band', split_axis=0, concat_axis=0, tiled=True)]
    sub x2 -> x0, other arithmetic: 27.8 us -> none  [on_device(): residual = residual - step_length * along]
    all_to_all x6 -> x0, local copies, waits for them, and re-layouts: 26.1 us -> none  [the longest x3 13.4 us: operate(): lax.all_to_all(returned, 'band', split_axis=0, concat_axis=3, tiled=True)]
    reduce_sum x0 -> x1, other arithmetic: none -> 24.7 us  [operate(): sums = lax.psum((jnp.sum(vector * vector), energy), 'field')]
    convert_element_type x6 -> x3, local copies, waits for them, and re-layouts: 18.9 us -> 0.92 us  [operate(): coeffs = lax.dot_general(masked_bf, legendre, (((2,), (1,)), ((0,), (0,))...]
  transfers between devices with their start and end apart: 1 -> 5, of which waited for: 1 -> 1; matrix products, arithmetic and copies ran while one was open for 2% -> 17% of each run, Pallas kernels for 0% -> 0%
where the time goes in v1:
time: 716 us; the launch traced here: 709 us
  blocking collectives  322 us (45%)
  matrix products  206 us (29%)
  other arithmetic  69.3 us (10%)
  local copies, waits for them, and re-layouts  45.3 us (6%)
  between operations  25.2 us (4%)
  starting transfers between devices  22.4 us (3%)
  waiting for transfers between devices  18.6 us (3%)
    psum x3, blocking collectives, operate(): norm, product = lax.psum(sums, 'band')  182 us
    all_to_all x2, blocking collectives, operate(): lax.all_to_all(outgoing, 'band', split_axis=0, concat_axis=0, tiled=True)  121 us
    dot_general x3, matrix products, operate(): lax.dot_general(home, legendre, (((2,), (2,)), ((0,), (0,))), preferred_e...  95.8 us
    dot_general x3, matrix products, operate(): lax.dot_general(masked_bf, legendre, (((2,), (1,)), ((0,), (0,))), prefer...  75.4 us
    cos x2, other arithmetic, fourier_phase(): jnp.cos(angles)  27.4 us
    reduce_sum x1, other arithmetic, operate(): sums = lax.psum((jnp.sum(vector * vector), energy), 'field')  24.7 us
    dot_general x3, matrix products, operate(): lax.dot_general(table_t, spread, (((1,), (0,)), ((), ())), preferred_elem...  19.9 us
    psum x3, blocking collectives, operate(): sums = lax.psum((jnp.sum(vector * vector), energy), 'field')  19.7 us
  transfers between devices with their start and end apart: 5, of which 1 were waited for; matrix products, arithmetic and copies ran while one was open for 17% of the time, Pallas kernels for 0%

profile of v1, /device:TPU:8, one launch (start us, length us, event | category | flops | bytes accessed | tf_op | source)
XLA Modules:
  0.0 709.2 jit_solution(14231911465912801690)
XLA Ops:
  7.2 0.7 all-gather.2.cloned.1.call-update
  7.9 0.8 dynamic_slice.6
  8.8 24.7 %multiply_reduce_fusion.5 = (f32[]{:T(128)}, f32[80,2,12,640]{3,2,1,0:T(8,128)}) fusion(f32[80,2,1,12,640]{4,2,3,1,0:T(1,128)} %param.4, f32[80,640]{1,0:T(8,128)S(1)} %fusion.33), kind=kLoop, calls=%fused_computation.24 | loop fusion | flops 3686399 | bytes 10035204 | tf_op jit(solution)/shard_map/reduce_sum | solution.py:176
  33.5 6.7 reshape.202
  40.1 25.0 %fusion.32 = bf16[80,24,640]{2,1,0:T(8,128)(2,1)S(1)} fusion(bf16[80,640,640]{2,1,0:T(8,128)(2,1)} %param.5, f32[80,24,640]{2,1,0:T(8,128)} %reshape.202, f32[80,640]{1,0:T(8,128)S(1)} %fusion.33), kind=kOutput, calls=%fused_computation.64 | convolution fusion | flops 1577779200 | bytes 73113600 | tf_op jit(solution)/shard_map/dot_general | solution.py:155
  65.2 0.3 copy.50
  66.0 0.4 maximum_bitcast_fusion.1
  66.6 1.8 copy.54
  68.4 6.7 all-to-all-start
  75.2 13.6 %fusion.8 = (f32[1280,8,1,80]{0,3,2,1:T(8,128)S(1)}, f32[1280,8,1,80]{0,3,2,1:T(8,128)S(1)}) fusion(s32[8,80]{1,0:T(8,128)S(1)} %mul.263), kind=kLoop, calls=%fused_computation.36 | loop fusion | flops 8192000 | bytes 6556160 | tf_op jit(solution)/shard_map/cos | solution.py:114
  88.8 2.4 fusion.1
  91.2 13.8 %fusion.11 = (f32[8,1,80,1280]{3,2,1,0:T(8,128)S(1)}, f32[8,1,80,1280]{3,2,1,0:T(8,128)S(1)}) fusion(s32[8,80]{1,0:T(8,128)S(1)} %mul.263), kind=kLoop, calls=%fused_computation.41 | loop fusion | flops 8192000 | bytes 6556160 | tf_op jit(solution)/shard_map/cos | solution.py:114
  105.0 2.4 fusion
  107.4 3.5 copy.56
  111.0 3.0 maximum_bitcast_fusion
  114.0 17.9 %all-to-all-done = bf16[8,160,1024]{2,1,0:T(8,128)(2,1)} async-done(((bf16[8,160,1024]{2,1,0:T(8,128)(2,1)}), bf16[8,160,1024]{2,1,0:T(8,128)(2,1)}, u32[]{:S(2)}, u32[]{:S(2)}) %all-to-all-start) | async-done | bytes 2621472 | tf_op jit(solution)/shard_map/all_to_all | solution.py:164
  131.9 9.7 %multiply_reduce_fusion.2 = (f32[]{:T(128)}, f32[1280,1024]{1,0:T(8,128)S(1)}) fusion(f32[1280,1024]{1,0:T(8,128)} %maximum_bitcast_fusion, f32[1024]{0:T(1024)S(1)} %fusion.36, bf16[1280,1280]{0,1:T(8,128)(2,1)} %bitcast.161, bf16[1280,1024]{1,0:T(8,128)(2,1)} %bitcast.12), kind=kOutput, calls=%fused_computation.7 | convolution fusion | flops 3360686080 | bytes 16388100 | tf_op jit(solution)/shard_map/dot_general | solution.py:166
  141.6 5.1 convolution_convert_fusion.2
  146.7 6.2 all-to-all-start.1
  152.9 7.1 %all-reduce.5 = (f32[]{:T(128)}, f32[]{:T(128)}) all-reduce(f32[]{:T(128)} %get-tuple-element.12, f32[]{:T(128)} %get-tuple-element.50), channel_id=1, replica_groups=mesh['band'=8,'field'=4] {'field'}, use_global_device_ids=true, to_apply=%region_1.2 | all-reduce | flops 2 | bytes 16 | tf_op jit(solution)/shard_map/psum | solution.py:176
  160.0 61.0 %all-reduce.2 = (f32[]{:T(128)}, f32[]{:T(128)}) all-reduce(f32[]{:T(128)} %get-tuple-element.24, f32[]{:T(128)} %get-tuple-element.25), channel_id=1, replica_groups=mesh['band'=8,'field'=4] {'band'}, use_global_device_ids=true, to_apply=%region_2.3 | all-reduce | flops 2 | bytes 16 | tf_op jit(solution)/shard_map/psum | solution.py:177
  223.4 0.3 pad_maximum_fusion.3
  224.0 32.3 %multiply_reduce_fusion.4 = (f32[]{:T(128)}, f32[80,24,640]{2,1,0:T(8,128)}, f32[80,24,640]{2,1,0:T(8,128)}) fusion(f32[]{:T(128)S(6)} %div.21, f32[80,24,640]{2,1,0:T(8,128)} %reshape.202, f32[80,640]{1,0:T(8,128)S(1)} %fusion.33, bf16[80,640,640]{2,1,0:T(8,128)(2,1)} %param.5, bf16[80,24,640]{2,0,1:T(8,128)(2,1)S(1)} %bitcast.131), kind=kOutput, calls=%fused_computation.18 | convolution fusion | flops 1581465600 | bytes 82944008 | tf_op jit(solution)/shard_map/dot_general | solution.py:186
  256.2 24.5 %fusion.31 = bf16[80,24,640]{2,1,0:T(8,128)(2,1)S(1)} fusion(bf16[80,640,640]{2,1,0:T(8,128)(2,1)} %param.5, f32[80,24,640]{2,1,0:T(8,128)} %get-tuple-element.27, f32[80,640]{1,0:T(8,128)S(1)} %fusion.33), kind=kOutput, calls=%fused_computation.63 | convolution fusion | flops 1576550400 | bytes 73113600 | tf_op jit(solution)/shard_map/dot_general | solution.py:155
  280.7 0.3 copy.60
  282.4 60.3 %all_to_all.30 = bf16[8,160,1024]{2,1,0:T(8,128)(2,1)S(1)} all-to-all(bf16[8,160,1024]{2,1,0:T(8,128)(2,1)S(1)} %bitcast.140), channel_id=1, replica_groups=mesh['band'=8,'field'=4] {'band'}, dimensions={0} | all-to-all | bytes 5242880 | tf_op jit(solution)/shard_map/all_to_all | solution.py:164
  342.7 5.1 multiply_reduce_fusion.1
  347.9 4.9 convolution_convert_fusion.1
  352.8 4.7 all-to-all-start.3
  357.5 6.3 all-reduce.4
  363.8 60.4 %all-reduce.1 = (f32[]{:T(128)}, f32[]{:T(128)}) all-reduce(f32[]{:T(128)} %get-tuple-element.22, f32[]{:T(128)} %get-tuple-element.23), channel_id=1, replica_groups=mesh['band'=8,'field'=4] {'band'}, use_global_device_ids=true, to_apply=%region_8.9 | all-reduce | flops 2 | bytes 16 | tf_op jit(solution)/shard_map/psum | solution.py:177
  428.9 0.3 pad_maximum_fusion.4
  429.4 32.5 %multiply_reduce_fusion.3 = (f32[]{:T(128)}, f32[80,24,640]{2,1,0:T(8,128)}) fusion(f32[80,24,640]{2,1,0:T(8,128)} %get-tuple-element.27, f32[]{:T(128)S(6)} %div.24, f32[80,24,640]{2,1,0:T(8,128)} %get-tuple-element.52, f32[80,24,640]{2,1,0:T(8,128)} %reshape.202, f32[]{:T(128)S(6)} %div.22, bf16[80,640,640]{2,1,0:T(8,128)(2,1)} %param.5, ...), kind=kOutput, calls=%fused_computation.14 | convolution fusion | flops 1586380800 | bytes 87859216 | tf_op jit(solution)/shard_map/dot_general | solution.py:186
  461.9 25.9 %fusion.30 = bf16[80,24,640]{2,1,0:T(8,128)(2,1)S(1)} fusion(bf16[80,640,640]{2,1,0:T(8,128)(2,1)} %param.5, f32[80,640]{1,0:T(8,128)S(1)} %fusion.33, f32[80,24,640]{2,1,0:T(8,128)} %get-tuple-element.27, f32[80,24,640]{2,1,0:T(8,128)} %get-tuple-element.56, f32[]{:T(128)S(6)} %div.24), kind=kOutput, calls=%fused_computation.62 | convolution fusion | flops 1579008000 | bytes 78028800 | tf_op jit(solution)/shard_map/dot_general | solution.py:155
  487.8 0.3 copy.68
  489.5 60.6 %all_to_all.31 = bf16[8,160,1024]{2,1,0:T(8,128)(2,1)S(1)} all-to-all(bf16[8,160,1024]{2,1,0:T(8,128)(2,1)S(1)} %bitcast.141), channel_id=1, replica_groups=mesh['band'=8,'field'=4] {'band'}, dimensions={0} | all-to-all | bytes 5242880 | tf_op jit(solution)/shard_map/all_to_all | solution.py:164
  550.1 5.1 multiply_reduce_fusion
  555.2 5.0 convolution_convert_fusion
  560.2 4.7 all-to-all-start.5
  564.9 6.3 all-reduce.3
  571.3 60.4 %all-reduce = (f32[]{:T(128)}, f32[]{:T(128)}) all-reduce(f32[]{:T(128)} %get-tuple-element.20, f32[]{:T(128)} %get-tuple-element.21), channel_id=1, replica_groups=mesh['band'=8,'field'=4] {'band'}, use_global_device_ids=true, to_apply=%region_14.15 | all-reduce | flops 2 | bytes 16 | tf_op jit(solution)/shard_map/psum | solution.py:177
  635.7 6.4 multiply_add_fusion
  642.1 3.1 copy.73
  645.2 9.7 %copy.78 = f32[80,2,1,12,640]{4,2,3,1,0:T(1,128)} copy(f32[80,2,1,12,640]{4,0,3,1,2:T(8,128)} %bitcast.129) | data formatting | bytes 9830400
  655.3 0.3 pad_maximum_fusion.5
  655.9 31.0 %multiply_subtract_fusion = f32[80,24,640]{2,1,0:T(8,128)} fusion(f32[80,24,640]{2,1,0:T(8,128)} %get-tuple-element.56, bf16[80,640,640]{2,1,0:T(8,128)(2,1)} %param.5, bf16[80,24,640]{2,0,1:T(8,128)(2,1)S(1)} %bitcast.132, f32[]{:T(128)S(6)} %div.25, f32[]{:T(128)S(6)} %div.27, f32[80,640]{1,0:T(8,128)S(1)} %fusion.33, ...), kind=kOutput, calls=%fused_computation.11 | convolution fusion | flops 1582694400 | bytes 82944016 | tf_op jit(solution)/shard_map/dot_general | solution.py:186
  686.9 5.5 copy.77
  692.4 9.7 %copy.79 = f32[80,2,1,12,640]{4,2,3,1,0:T(1,128)} copy(f32[80,2,1,12,640]{4,0,3,1,2:T(8,128)} %bitcast.130) | data formatting | bytes 9830400
  (66 shorter events, 5.4 us)
Async XLA Ops:
  7.2 100.2 %all-gather.2.cloned.1.call-start = ((), (), s32[]{:S(2)}) async-start(), calls=%async_computation.6 | async-start | bytes 3686400 | tf_op jit(solution)/shard_map/all_gather | solution.py:145
  68.4 6.7 copy-start.6
  68.4 63.6 %all-to-all-start = ((bf16[8,160,1024]{2,1,0:T(8,128)(2,1)}), bf16[8,160,1024]{2,1,0:T(8,128)(2,1)}, u32[]{:S(2)}, u32[]{:S(2)}) async-start(bf16[8,160,1024]{2,1,0:T(8,128)(2,1)} %bitcast.11), calls=%async_computation | async-start | bytes 5242880 | tf_op jit(solution)/shard_map/all_to_all | solution.py:164
  131.9 9.7 %copy-start = (f32[1280,1024]{1,0:T(8,128)S(1)}, f32[1280,1024]{1,0:T(8,128)}, u32[]{:S(2)}) copy-start(f32[1280,1024]{1,0:T(8,128)} %maximum_bitcast_fusion) | copy-start | bytes 15728644
  131.9 9.7 %copy-start.3 = (bf16[8,2,80,1280]{3,2,1,0:T(8,128)(2,1)S(1)}, bf16[8,2,80,1280]{3,2,1,0:T(8,128)(2,1)}, u32[]{:S(2)}) copy-start(bf16[8,2,80,1280]{3,2,1,0:T(8,128)(2,1)} %fusion) | copy-start | bytes 9830404
  146.7 76.3 %all-to-all-start.1 = ((bf16[8,160,1024]{2,1,0:T(8,128)(2,1)}), bf16[8,160,1024]{2,1,0:T(8,128)(2,1)S(1)}, u32[]{:S(2)}, u32[]{:S(2)}) async-start(bf16[8,160,1024]{2,1,0:T(8,128)(2,1)} %bitcast.169), calls=%async_computation.1 | async-start | bytes 5242880 | tf_op jit(solution)/shard_map/all_to_all | solution.py:178
  281.9 60.8 %slice-start = ((s8[5242880]{0:T(1024)(128)(4,1)}), s8[4194304]{0:T(1024)(128)(4,1)S(1)}, s32[]{:S(2)}) async-start(s8[5242880]{0:T(1024)(128)(4,1)} %bitcast.157), calls=%async_computation.7 | async-start | bytes 8388608
  282.1 60.6 %slice-start.1 = ((s8[5242880]{0:T(1024)(128)(4,1)}), s8[1048576]{0:T(1024)(128)(4,1)S(1)}, s32[]{:S(2)}) async-start(s8[5242880]{0:T(1024)(128)(4,1)} %bitcast.157), calls=%async_computation.8 | async-start | bytes 2097152
  282.4 60.3 %copy-start.1 = (bf16[1280,8,2,80]{0,3,2,1:T(8,128)(2,1)S(1)}, bf16[1280,8,2,80]{0,3,2,1:T(8,128)(2,1)}, u32[]{:S(2)}) copy-start(bf16[1280,8,2,80]{0,3,2,1:T(8,128)(2,1)} %fusion.1) | copy-start | bytes 9830404
  342.7 5.2 copy-start.4
  352.8 75.7 %all-to-all-start.3 = ((bf16[8,160,1024]{2,1,0:T(8,128)(2,1)}), bf16[8,160,1024]{2,1,0:T(8,128)(2,1)S(1)}, u32[]{:S(2)}, u32[]{:S(2)}) async-start(bf16[8,160,1024]{2,1,0:T(8,128)(2,1)} %bitcast.168), calls=%async_computation.3 | async-start | bytes 5242880 | tf_op jit(solution)/shard_map/all_to_all | solution.py:178
  489.0 61.1 %slice-start.2 = ((s8[5242880]{0:T(1024)(128)(4,1)}), s8[4194304]{0:T(1024)(128)(4,1)S(1)}, s32[]{:S(2)}) async-start(s8[5242880]{0:T(1024)(128)(4,1)} %bitcast.159), calls=%async_computation.9 | async-start | bytes 8388608
  489.2 60.8 %slice-start.3 = ((s8[5242880]{0:T(1024)(128)(4,1)}), s8[1048576]{0:T(1024)(128)(4,1)S(1)}, s32[]{:S(2)}) async-start(s8[5242880]{0:T(1024)(128)(4,1)} %bitcast.159), calls=%async_computation.10 | async-start | bytes 2097152
  489.5 60.6 %copy-start.2 = (bf16[1280,8,2,80]{0,3,2,1:T(8,128)(2,1)S(1)}, bf16[1280,8,2,80]{0,3,2,1:T(8,128)(2,1)}, u32[]{:S(2)}) copy-start(bf16[1280,8,2,80]{0,3,2,1:T(8,128)(2,1)} %fusion.1) | copy-start | bytes 9830404
  550.1 5.1 copy-start.5
  560.2 94.7 %all-to-all-start.5 = ((bf16[8,160,1024]{2,1,0:T(8,128)(2,1)}), bf16[8,160,1024]{2,1,0:T(8,128)(2,1)S(1)}, u32[]{:S(2)}, u32[]{:S(2)}) async-start(bf16[8,160,1024]{2,1,0:T(8,128)(2,1)} %bitcast.167), calls=%async_computation.5 | async-start | bytes 5242880 | tf_op jit(solution)/shard_map/all_to_all | solution.py:178
Sparse Core Ops, SparseCore 0:
  10.2 62.5 all-gather.1
